TPU v7x, 32 devices: a whole 2x2x4 slice. The times are simulated.
32 devices in a mesh: section: 4 (over y, core), fsdp: 8 (over z, x).
Axes of the slice: x: 2, y: 2, z: 4, core: 2. Of those that a mesh axis runs over, the one named last changes fastest.
Arguments:
- old_pieces: bfloat16 [4, 2, 16384, 1024], P('section', None, 'fsdp'), may hold values from -0.0625 to 0.0625
- section_inputs: bfloat16 [4, 4096, 8192], P('section', 'fsdp'), may hold values from -6 to 6
- old_section_of: int32 [8], replicated, may hold values from 0 to 3, as said below
- new_section_of: int32 [8], replicated, may hold values from 0 to 7, as said below
- old_order: int32 [8, 2], replicated, may hold values from 0 to 1, each once within a row
- new_order: int32 [8, 2], replicated, may hold values from 0 to 1, each once within a row
Outputs:
- new_shards: bfloat16 [4, 32768, 1024], P('section', 'fsdp')
- kv_out: bfloat16 [4, 4096, 2048], P('section', 'fsdp')
Inputs may be any that keep to these rules, and one draw needn't show every extreme that they name: `old_section_of`: each old section holds exactly two layers. Each new section holds exactly one layer; the two layers of one old section have different values of new_section_of // 2.
All inputs are finite; a program needn't handle non-finite values.
Results may differ from a plain program's by a relative error of at most 0.001.
Values may be sent and summed in bfloat16 or wider, within the bound.
A program may use at most 192 MiB of HBM per device.

v0:
```python
import math

import jax
import jax.numpy as jnp
from jax import lax
from jax.sharding import PartitionSpec as P

HEAD_DIM = 128


def from_partner(block, axis, stride):
    count = lax.axis_size(axis)
    route = []
    for low in range(count):
        high = low | 1 << stride
        if high != low and high < count:
            route += [(low, high), (high, low)]
    return lax.ppermute(block, axis, route)


def rotate_keys(values, positions):
    tok_rows = values.shape[0]
    heads = values.reshape(tok_rows, -1, HEAD_DIM)
    half_dim = HEAD_DIM // 2
    freq_index = jnp.arange(half_dim, dtype=jnp.float32)
    inverse_freq = jnp.exp(freq_index * (-2.0 * math.log(500000.0) / HEAD_DIM))
    angles = positions.astype(jnp.float32)[:, None] * inverse_freq[None, :]
    cosine = jnp.cos(angles)[:, None, :]
    sine = jnp.sin(angles)[:, None, :]
    lower = heads[..., :half_dim]
    upper = heads[..., half_dim:]
    turned = jnp.concatenate(
        [lower * cosine - upper * sine, upper * cosine + lower * sine], axis=-1
    )
    return turned.reshape(tok_rows, -1)


def pick_entry(table, index_value):
    positions = jnp.arange(table.shape[0], dtype=jnp.int32)
    return jnp.sum(jnp.where(positions == index_value, table, 0))


def pick_row(table, index_value):
    positions = jnp.arange(table.shape[0], dtype=jnp.int32)[:, None]
    return jnp.sum(jnp.where(positions == index_value, table, 0), axis=0)


def per_device(old_pieces, section_inputs, old_section_of, new_section_of, old_order, new_order):
    section_count = lax.axis_size("section")
    member_count = lax.axis_size("fsdp")
    digit_count = member_count.bit_length() - 1
    row_index = lax.axis_index("section")
    member = lax.axis_index("fsdp")
    parity = member % 2
    layer_total = old_section_of.shape[0]
    layer_ids = jnp.arange(layer_total, dtype=jnp.int32)
    in_row = old_section_of == row_index
    layer_low = jnp.min(jnp.where(in_row, layer_ids, layer_total))
    layer_high = jnp.max(jnp.where(in_row, layer_ids, -1))
    target_low = pick_entry(new_section_of, layer_low) // 2
    target_high = pick_entry(new_section_of, layer_high) // 2
    pieces = old_pieces[0]
    targets = jnp.arange(section_count, dtype=jnp.int32)[:, None, None]
    nothing = jnp.zeros_like(pieces[0])
    outgoing = jnp.where(
        targets == target_low,
        pieces[0][None],
        jnp.where(targets == target_high, pieces[1][None], nothing[None]),
    )
    incoming = lax.all_to_all(outgoing, "section", split_axis=0, concat_axis=0, tiled=True)
    layer_own = jnp.sum(jnp.where(new_section_of == 2 * row_index + parity, layer_ids, 0))
    layer_foreign = jnp.sum(jnp.where(new_section_of == 2 * row_index + 1 - parity, layer_ids, 0))
    own_piece = lax.dynamic_index_in_dim(
        incoming, pick_entry(old_section_of, layer_own), 0, keepdims=False
    )
    foreign_piece = lax.dynamic_index_in_dim(
        incoming, pick_entry(old_section_of, layer_foreign), 0, keepdims=False
    )
    partner_piece = from_partner(foreign_piece, "fsdp", 0)
    lower = jnp.where(parity == 0, own_piece, partner_piece)
    upper = jnp.where(parity == 0, partner_piece, own_piece)
    holding = jnp.concatenate([lower, upper], axis=0)
    tokens = section_inputs[0]
    tok_rows, model_width = tokens.shape
    shard_rows, kv_width = holding.shape
    own_bits = {digit: member // 2**digit % 2 for digit in range(1, digit_count)}
    own_old = pick_row(old_order, layer_own)
    own_new = pick_row(new_order, layer_own)
    flipped = own_old[0] != own_new[0]
    group_digits = digit_count - 1
    low_count = group_digits // 2
    high_digits = list(range(low_count + 1, digit_count))
    low_digits = list(range(1, low_count + 1))
    gathered = holding
    digits_done = []
    for digit in high_digits:
        received = from_partner(gathered, "fsdp", digit)
        bit_value = own_bits[digit]
        lower = jnp.where(bit_value == 0, gathered, received)
        upper = jnp.where(bit_value == 0, received, gathered)
        position = len([other_digit for other_digit in digits_done if other_digit > digit])
        gathered = jnp.stack([lower, upper], axis=position)
        digits_done = sorted(digits_done + [digit], reverse=True)
    weight_blocks = gathered.reshape(2, -1, shard_rows, kv_width)
    block_count = weight_blocks.shape[1]
    column_view = tokens.reshape((tok_rows, block_count) + (2,) * low_count + (shard_rows,))
    for digit in low_digits:
        axis_index = 2 + (low_count - digit)
        bit_value = own_bits[digit]
        mine = lax.dynamic_index_in_dim(column_view, bit_value, axis_index, keepdims=False)
        other = lax.dynamic_index_in_dim(column_view, 1 - bit_value, axis_index, keepdims=False)
        received = from_partner(other, "fsdp", digit)
        lower = jnp.where(bit_value == 0, mine, received)
        upper = jnp.where(bit_value == 0, received, mine)
        column_view = jnp.stack([lower, upper], axis=axis_index)
    token_blocks = column_view.reshape(tok_rows, block_count, 2**low_count, shard_rows)
    partial_value = jnp.einsum(
        "tabi,saik->sbtk", token_blocks, weight_blocks, preferred_element_type=jnp.float32
    )
    partial_value = partial_value.reshape((2,) + (2,) * low_count + (tok_rows, kv_width))
    for digit in low_digits:
        axis_index = 1 + (low_count - digit)
        bit_value = own_bits[digit]
        mine = lax.dynamic_index_in_dim(partial_value, bit_value, axis_index, keepdims=True)
        other = lax.dynamic_index_in_dim(partial_value, 1 - bit_value, axis_index, keepdims=True)
        received = from_partner(other, "fsdp", digit)
        partial_value = mine + received
    totals = partial_value.reshape(2, tok_rows, kv_width)
    top_bit = own_bits[digit_count - 1]
    matrix_index = jnp.where(flipped, 1 - top_bit, top_bit)
    block_index = member // 2 // 2**low_count % block_count
    chosen_matrix = lax.dynamic_index_in_dim(weight_blocks, matrix_index, 0, keepdims=False)
    new_shard = lax.dynamic_index_in_dim(chosen_matrix, block_index, 0, keepdims=False)
    keys = jnp.where(own_old[0] == 0, totals[0], totals[1])
    values = jnp.where(own_old[1] == 0, totals[0], totals[1])
    positions = member // 2 * tok_rows + jnp.arange(tok_rows, dtype=jnp.int32)
    joined = jnp.concatenate([rotate_keys(keys, positions), values], axis=-1).astype(jnp.bfloat16)
    return (new_shard[None], joined[None])


def solution(mesh):
    in_specs = (P("section", None, "fsdp", None), P("section", "fsdp", None), P(), P(), P(), P())
    out_specs = (P("section", "fsdp", None), P("section", "fsdp", None))
    return jax.shard_map(
        per_device, mesh=mesh, in_specs=in_specs, out_specs=out_specs, check_vma=False
    )
```

profile of v0, /device:TPU:0, one launch (start us, length us, event | category | flops | bytes accessed | tf_op | source)
XLA Modules:
  0.0 845.5 jit_solution(6211819698377527555)
XLA Ops:
  12.2 6.1 slice_bitcast_fusion.1
  18.3 6.5 copy.8
  24.8 6.4 copy.9
  31.2 10.8 %select_select_fusion = bf16[4,2048,1024]{1,2,0:T(8,128)(2,1)} fusion(pred[4]{0:T(512)(128)(4,1)S(1)} %get-tuple-element.30, pred[4]{0:T(512)(128)(4,1)S(1)} %get-tuple-element.31, bf16[2048,1024]{0,1:T(8,128)(2,1)} %copy.9, bf16[2048,1024]{0,1:T(8,128)(2,1)} %copy.8), kind=kLoop, calls=%fused_computation.5 | loop fusion | flops 16777216 | bytes 25165832 | tf_op jit(solution)/shard_map/jit(_where)/select_n | solution.py:65
  42.0 7.0 all-to-all-start
  51.1 181.7 %all-to-all-done = bf16[4,2048,1024]{1,2,0:T(8,128)(2,1)} async-done(((bf16[4,2048,1024]{1,2,0:T(8,128)(2,1)}), bf16[4,2048,1024]{1,2,0:T(8,128)(2,1)}, u32[]{:S(2)}, u32[]{:S(2)}) %all-to-all-start) | async-done | bytes 16777248 | tf_op jit(solution)/shard_map/all_to_all | solution.py:70
  232.7 4.8 dynamic-slice_bitcast_fusion.1
  241.6 88.8 %collective-permute-done = bf16[2048,1024]{0,1:T(8,128)(2,1)} collective-permute-done((bf16[2048,1024]{0,1:T(8,128)(2,1)}, bf16[2048,1024]{0,1:T(8,128)(2,1)}, u32[]{:S(2)}, u32[]{:S(2)}) %collective-permute-start) | collective-permute-done | bytes 4194336 | tf_op jit(solution)/shard_map/ppermute | solution.py:18
  330.3 5.7 bitcast_select_fusion.1
  336.0 8.0 pad_maximum_fusion.1
  344.0 2.8 collective-permute-start.1
  346.9 14.4 %reshape_squeeze.3 = bf16[512,1,2,4096]{3,2,0,1:T(2,128)(2,1)} reshape(bf16[1,512,8192]{2,1,0:T(8,128)(2,1)} %param.7) | data formatting | bytes 16777216 | tf_op jit(solution)/shard_map/reshape;squeeze | solution.py:106
  361.3 20.4 %constant_dynamic-slice_fusion.1 = (bf16[512,1,1,4096]{3,2,0,1:T(2,128)(2,1)}, bf16[512,1,1,4096]{3,2,0,1:T(2,128)(2,1)S(1)}) fusion(bf16[512,1,2,4096]{3,2,0,1:T(2,128)(2,1)} %reshape_squeeze.3, s32[]{:T(128)S(6)} %select_n.191, s32[]{:T(128)S(6)} %select_n.192), kind=kLoop, calls=%fused_computation.35 | loop fusion | bytes 16777224 | tf_op jit(solution)/shard_map/jit(dynamic_index_in_dim)/dynamic_slice | solution.py:110
  381.7 6.7 copy.23
  390.0 225.7 %collective-permute-done.2 = bf16[512,1,4096]{2,0,1:T(8,128)(2,1)} collective-permute-done((bf16[512,1,4096]{2,0,1:T(8,128)(2,1)}, bf16[512,1,4096]{2,0,1:T(8,128)(2,1)}, u32[]{:S(2)}, u32[]{:S(2)}) %collective-permute-start.2) | collective-permute-done | bytes 4194336 | tf_op jit(solution)/shard_map/ppermute | solution.py:18
  615.7 10.8 %select_bitcast_fusion.3 = (bf16[512,1,1,4096]{3,0,2,1:T(8,128)(2,1)S(1)}, bf16[512,1,1,4096]{3,0,2,1:T(8,128)(2,1)}) fusion(bf16[512,1,4096]{2,0,1:T(8,128)(2,1)} %collective-permute-done.2, pred[]{:T(512)S(6)} %eq.124, bf16[512,1,1,4096]{3,2,0,1:T(2,128)(2,1)} %get-tuple-element.20), kind=kLoop, calls=%fused_computation.20 | loop fusion | flops 4194304 | bytes 16777216 | tf_op jit(solution)/shard_map/stack | solution.py:115
  626.4 79.9 %collective-permute-done.1 = bf16[4096,1024]{0,1:T(8,128)(2,1)} collective-permute-done((bf16[4096,1024]{0,1:T(8,128)(2,1)}, bf16[4096,1024]{0,1:T(8,128)(2,1)}, u32[]{:S(2)}, u32[]{:S(2)}) %collective-permute-start.1) | collective-permute-done | bytes 8388640 | tf_op jit(solution)/shard_map/ppermute | solution.py:18
  706.3 11.1 %select_bitcast_fusion = (bf16[1,4096,1024]{1,2,0:T(8,128)(2,1)}, bf16[1,4096,1024]{1,2,0:T(8,128)(2,1)}) fusion(bf16[4096,1024]{0,1:T(8,128)(2,1)} %collective-permute-done.1, pred[]{:T(512)S(6)} %eq.102, bf16[2048,1024]{0,1:T(8,128)(2,1)S(1)} %copy-done.1, bf16[2048,1024]{0,1:T(8,128)(2,1)S(1)} %copy-done), kind=kLoop, calls=%fused_computation.11 | loop fusion | flops 25165824 | bytes 33554432 | tf_op jit(solution)/shard_map/stack | solution.py:102
  717.5 23.5 %fusion.1 = f32[2,1024,512,2]{2,1,3,0:T(8,128)} fusion(bf16[1,4096,1024]{1,2,0:T(8,128)(2,1)} %get-tuple-element.16, bf16[1,4096,1024]{1,2,0:T(8,128)(2,1)} %get-tuple-element.17, bf16[512,1,1,4096]{3,0,2,1:T(8,128)(2,1)} %get-tuple-element.19, bf16[512,1,1,4096]{3,0,2,1:T(8,128)(2,1)S(1)} %get-tuple-element.18), kind=kOutput, calls=%fused_computation.4 | convolution fusion | flops 17230200832 | bytes 33554432 | tf_op jit(solution)/shard_map/tabi,saik->sbtk/dot_general | solution.py:117
  740.9 4.6 dynamic-slice_bitcast_fusion
  750.0 8.3 fusion.3
  758.3 11.9 %copy.12 = bf16[1,4096,1024]{2,1,0:T(8,128)(2,1)} copy(bf16[1,4096,1024]{1,2,0:T(8,128)(2,1)} %fusion.3) | data formatting | bytes 16777216
  770.2 67.1 %collective-permute-done.3 = f32[2,1,512,1024]{2,3,1,0:T(8,128)} collective-permute-done((f32[2,1,512,1024]{2,3,1,0:T(8,128)}, f32[2,1,512,1024]{2,3,1,0:T(8,128)}, u32[]{:S(2)}, u32[]{:S(2)}) %collective-permute-start.3) | collective-permute-done | bytes 4194336 | tf_op jit(solution)/shard_map/ppermute | solution.py:18
  837.4 4.5 bitcast_add_fusion
  (27 shorter events, 16.8 us)
Async XLA Ops:
  42.0 190.7 %all-to-all-start = ((bf16[4,2048,1024]{1,2,0:T(8,128)(2,1)}), bf16[4,2048,1024]{1,2,0:T(8,128)(2,1)}, u32[]{:S(2)}, u32[]{:S(2)}) async-start(bf16[4,2048,1024]{1,2,0:T(8,128)(2,1)} %select_select_fusion), calls=%async_computation | async-start | bytes 33554432 | tf_op jit(solution)/shard_map/all_to_all | solution.py:70
  237.5 92.8 %collective-permute-start = (bf16[2048,1024]{0,1:T(8,128)(2,1)}, bf16[2048,1024]{0,1:T(8,128)(2,1)}, u32[]{:S(2)}, u32[]{:S(2)}) collective-permute-start(bf16[2048,1024]{0,1:T(8,128)(2,1)} %dynamic-slice_bitcast_fusion.1), channel_id=1, source_target_pairs={{0,1},{1,0},{2,3},{3,2},{4,5},{5,4},{6,7},{7,6},{8,9},{9,8},{10,11... | collective-permute-start | bytes 12582920 | tf_op jit(solution)/shard_map/ppermute | solution.py:18
  344.0 362.3 %collective-permute-start.1 = (bf16[4096,1024]{0,1:T(8,128)(2,1)}, bf16[4096,1024]{0,1:T(8,128)(2,1)}, u32[]{:S(2)}, u32[]{:S(2)}) collective-permute-start(bf16[4096,1024]{0,1:T(8,128)(2,1)} %pad_maximum_fusion.1), channel_id=1, source_target_pairs={{0,4},{4,0},{1,5},{5,1},{2,6},{6,2},{3,7},{7,3},{8,12},{12,8},{9,1... | collective-permute-start | bytes 25165832 | tf_op jit(solution)/shard_map/ppermute | solution.py:18
  388.4 227.3 %collective-permute-start.2 = (bf16[512,1,4096]{2,0,1:T(8,128)(2,1)}, bf16[512,1,4096]{2,0,1:T(8,128)(2,1)}, u32[]{:S(2)}, u32[]{:S(2)}) collective-permute-start(bf16[512,1,4096]{2,0,1:T(8,128)(2,1)} %bitcast.45), channel_id=1, source_target_pairs={{0,2},{2,0},{1,3},{3,1},{4,6},{6,4},{5,7},{7,5},{8,10},{10,8},{9,1... | collective-permute-start | bytes 12582920 | tf_op jit(solution)/shard_map/ppermute | solution.py:18
  615.7 90.7 %copy-start = (bf16[2048,1024]{0,1:T(8,128)(2,1)S(1)}, bf16[2048,1024]{0,1:T(8,128)(2,1)}, u32[]{:S(2)}) copy-start(bf16[2048,1024]{0,1:T(8,128)(2,1)} %get-tuple-element.14) | copy-start | bytes 12582916
  615.7 90.7 %copy-start.1 = (bf16[2048,1024]{0,1:T(8,128)(2,1)S(1)}, bf16[2048,1024]{0,1:T(8,128)(2,1)}, u32[]{:S(2)}) copy-start(bf16[2048,1024]{0,1:T(8,128)(2,1)} %get-tuple-element.15) | copy-start | bytes 12582916
  740.9 5.9 copy-start.2
  740.9 5.9 copy-start.3
  745.5 91.8 %collective-permute-start.3 = (f32[2,1,512,1024]{2,3,1,0:T(8,128)}, f32[2,1,512,1024]{2,3,1,0:T(8,128)}, u32[]{:S(2)}, u32[]{:S(2)}) collective-permute-start(f32[2,1,512,1024]{2,3,1,0:T(8,128)} %dynamic-slice_bitcast_fusion), channel_id=1, source_target_pairs={{0,2},{2,0},{1,3},{3,1},{4,6},{6,4},{5,7},{7,5},{8,10},{10,8},{9,1... | collective-permute-start | bytes 12582920 | tf_op jit(solution)/shard_map/ppermute | solution.py:18
where the time goes:
time: 847 us; the launch traced here: 845 us
  waiting for transfers between devices  643 us (76%)
  local copies, waits for them, and re-layouts  84.8 us (10%)
  other arithmetic  68.5 us (8%)
  matrix products  23.5 us (3%)
  starting transfers between devices  14.3 us (2%)
  between operations  11.3 us (1%)
    ppermute x4, waiting for transfers between devices, from_partner(): return lax.ppermute(block, axis, route)  461 us
    all_to_all x1, waiting for transfers between devices, per_device(): lax.all_to_all(outgoing, 'section', split_axis=0, concat_axis=0, tiled=True)  182 us
    dot_general x1, matrix products, per_device(): jnp.einsum('tabi,saik->sbtk', token_blocks, weight_blocks, preferred_elem...  23.5 us
    unnamed x11, local copies, waits for them, and re-layouts  21 us
    dynamic_slice x1, local copies, waits for them, and re-layouts, per_device(): lax.dynamic_index_in_dim(column_view, bit_value, axis_index, keepdims=False)  20.4 us
    another operation x2, other arithmetic, per_device(): gathered = jnp.stack([lower, upper], axis=position)  19.5 us
  transfers between devices with their start and end apart: 5, of which 5 were waited for; matrix products, arithmetic and copies ran while one was open for 9% of the time, Pallas kernels for 0%

commit v1 on v0

v1 whole, which is shorter than its diff:
```python
import math

import jax
import jax.numpy as jnp
from jax import lax
from jax.sharding import PartitionSpec as P


HEAD_DIM = 128


def from_partner(block, axis, stride):
    count = lax.axis_size(axis)
    route = []
    for low in range(count):
        high = low | 1 << stride
        if high != low and high < count:
            route += [(low, high), (high, low)]
    return lax.ppermute(block, axis, route)


def from_offset(block, axis, offset):
    count = lax.axis_size(axis)
    return lax.ppermute(block, axis, [(i, i ^ offset) for i in range(count)])


def rotate_keys(values, positions):
    tok_rows = values.shape[0]
    heads = values.reshape(tok_rows, -1, HEAD_DIM)
    half_dim = HEAD_DIM // 2
    freq_index = jnp.arange(half_dim, dtype=jnp.float32)
    inverse_freq = jnp.exp(freq_index * (-2.0 * math.log(500000.0) / HEAD_DIM))
    angles = positions.astype(jnp.float32)[:, None] * inverse_freq[None, :]
    cosine = jnp.cos(angles)[:, None, :]
    sine = jnp.sin(angles)[:, None, :]
    lower = heads[..., :half_dim]
    upper = heads[..., half_dim:]
    turned = jnp.concatenate(
        [lower * cosine - upper * sine, upper * cosine + lower * sine], axis=-1
    )
    return turned.reshape(tok_rows, -1)


def pick_entry(table, index_value):
    positions = jnp.arange(table.shape[0], dtype=jnp.int32)
    return jnp.sum(jnp.where(positions == index_value, table, 0))


def pick_row(table, index_value):
    positions = jnp.arange(table.shape[0], dtype=jnp.int32)[:, None]
    return jnp.sum(jnp.where(positions == index_value, table, 0), axis=0)


def chunk_columns(kv_width):
    heads = kv_width // HEAD_DIM
    edge = [1, 1] if heads >= 4 else []
    middle = heads - len(edge)
    sizes = [2] * (middle // 2) + [1] * (middle % 2) + edge
    starts = [sum(sizes[:i]) for i in range(len(sizes))]
    return [(s * HEAD_DIM, n * HEAD_DIM) for s, n in zip(starts, sizes)]


def per_device(old_pieces, section_inputs, old_section_of, new_section_of, old_order, new_order):
    section_count = lax.axis_size("section")
    member_count = lax.axis_size("fsdp")
    digit_count = member_count.bit_length() - 1
    row_index = lax.axis_index("section")
    member = lax.axis_index("fsdp")
    parity = member % 2
    layer_total = old_section_of.shape[0]
    layer_ids = jnp.arange(layer_total, dtype=jnp.int32)
    in_row = old_section_of == row_index
    layer_low = jnp.min(jnp.where(in_row, layer_ids, layer_total))
    layer_high = jnp.max(jnp.where(in_row, layer_ids, -1))
    target_low = pick_entry(new_section_of, layer_low) // 2
    layer_own = jnp.sum(jnp.where(new_section_of == 2 * row_index + parity, layer_ids, 0))
    layer_foreign = jnp.sum(jnp.where(new_section_of == 2 * row_index + 1 - parity, layer_ids, 0))
    source_own = pick_entry(old_section_of, layer_own)
    source_foreign = pick_entry(old_section_of, layer_foreign)
    pieces = old_pieces[0]
    tokens = section_inputs[0]
    tok_rows, _ = tokens.shape
    shard_rows, kv_width = 2 * pieces.shape[1], pieces.shape[2]
    own_bits = {digit: member // 2**digit % 2 for digit in range(1, digit_count)}
    own_old = pick_row(old_order, layer_own)
    own_new = pick_row(new_order, layer_own)
    flipped = own_old[0] != own_new[0]
    group_digits = digit_count - 1
    low_count = group_digits // 2
    high_digits = list(range(low_count + 1, digit_count))
    low_digits = list(range(1, low_count + 1))
    top_bit = own_bits[digit_count - 1]

    def to_groups(low, high):
        sources = []
        for offset in range(section_count):
            chosen = jnp.where(target_low == row_index ^ offset, low, high)
            if offset:
                chosen = from_offset(chosen, "section", offset)
            sources.append(chosen)
        (own_from, foreign_from, here, side), sources = lax.optimization_barrier(
            ((source_own, source_foreign, row_index, parity), sources)
        )
        own, foreign = sources[0], sources[0]
        for offset in range(1, section_count):
            own = jnp.where(own_from == here ^ offset, sources[offset], own)
            foreign = jnp.where(foreign_from == here ^ offset, sources[offset], foreign)
        partner = from_partner(foreign, "fsdp", 0)
        lower = jnp.where(side == 0, own, partner)
        upper = jnp.where(side == 0, partner, own)
        return jnp.concatenate([lower, upper], axis=-2)

    def gather_high(block):
        blocks = [block]
        for digit in high_digits:
            blocks += [from_partner(held, "fsdp", digit) for held in blocks]
        return blocks

    block_digits = high_digits[:-1]
    place_digits = block_digits[::-1] + low_digits[::-1]

    def pick_columns(flips):
        column = 0
        for digit in place_digits:
            column = 2 * column + (own_bits[digit] ^ flips[digit])
        return lax.dynamic_slice_in_dim(tokens, column * shard_rows, shard_rows, axis=1)

    row_cuts = 4 if tok_rows % 64 == 0 else 1
    token_blocks = {}
    for number in range(2 ** len(block_digits)):
        flips = {digit: number >> place & 1 for place, digit in enumerate(block_digits)}
        pending = {}
        for want in range(2**low_count):
            low_flips = {digit: want >> place & 1 for place, digit in enumerate(low_digits)}
            pending[want] = pick_columns({**flips, **low_flips})
        for place, digit in enumerate(low_digits):
            moved = dict(pending)
            for want in range(2**low_count):
                if want >> place & 1:
                    cuts = jnp.split(pending[want], row_cuts, axis=0)
                    cuts = [from_partner(cut, "fsdp", digit) for cut in cuts]
                    moved[want] = jnp.concatenate(cuts, axis=0)
            pending = moved
        for want in range(2**low_count):
            token_blocks[want, number] = pending[want]

    def project(blocks):
        sums = []
        for want in reversed(range(2**low_count)):
            for number, block in enumerate(blocks):
                product = jnp.dot(
                    token_blocks[want, number], block, preferred_element_type=jnp.float32
                )
                total = total + product if number else product
            sums.append(total)
        sums = sums[::-1]
        for place in reversed(range(low_count)):
            half = len(sums) // 2
            sums = [
                kept + from_partner(sent, "fsdp", low_digits[place])
                for kept, sent in zip(sums[:half], sums[half:])
            ]
        return sums[0]

    positions = member // 2 * tok_rows + jnp.arange(tok_rows, dtype=jnp.int32)
    shard_parts, key_parts, value_parts = [], [], []
    for number, (start, width) in enumerate(chunk_columns(kv_width)):
        part = lax.slice_in_dim(pieces, start, start + width, axis=2)
        if number == 0:
            crossed = jnp.stack(gather_high(part), axis=1)
            held = to_groups(crossed[0], crossed[1])
            blocks = [held[i] for i in range(held.shape[0])]
        else:
            blocks = gather_high(to_groups(part[0], part[1]))
        half = len(blocks) // 2
        near = project(blocks[:half])
        far = project(blocks[half:])
        shard_parts.append(jnp.where(flipped, blocks[half], blocks[0]))
        keys = jnp.where(own_old[0] == top_bit, near, far)
        values = jnp.where(own_old[1] == top_bit, near, far)
        key_parts.append(rotate_keys(keys, positions).astype(jnp.bfloat16))
        value_parts.append(values.astype(jnp.bfloat16))
    new_shard = jnp.concatenate(shard_parts, axis=1)
    joined = jnp.concatenate(key_parts + value_parts, axis=1)
    return (new_shard[None], joined[None])


def solution(mesh):
    in_specs = (P("section", None, "fsdp", None), P("section", "fsdp", None), P(), P(), P(), P())
    out_specs = (P("section", "fsdp", None), P("section", "fsdp", None))

    return jax.shard_map(
        per_device, mesh=mesh, in_specs=in_specs, out_specs=out_specs, check_vma=False
    )
```

time: 847 us -> 568 us (0.67); the launches traced: 845 us -> 557 us
  waiting for transfers between devices: 643 us -> 354 us
  local copies, waits for them, and re-layouts: 84.8 us -> 22 us
  matrix products: 23.5 us -> 55.5 us
  starting transfers between devices: 14.3 us -> 45.7 us
  between operations: 11.3 us -> 26.1 us
  other arithmetic: 68.5 us -> 54.1 us
    all_to_all x1 -> x0, waiting for transfers between devices: 182 us -> none  [per_device(): lax.all_to_all(outgoing, 'section', split_axis=0, concat_axis=0, tiled=True)]
    ppermute x4 -> x24, waiting for transfers between devices: 461 us -> 285 us  [from_partner(): return lax.ppermute(block, axis, route)]
    ppermute x0 -> x15, waiting for transfers between devices: none -> 68.7 us  [from_offset(): return lax.ppermute(block, axis, [(i, i ^ offset) for i in range(count)])]
    dot_general x1 -> x20, matrix products: 23.5 us -> 55.5 us  [project(): jnp.dot(token_blocks[want, number], block, preferred_element_type=jnp.flo...]
    another operation x4 -> x2, other arithmetic: 30.6 us -> 1.55 us  [the longest x2 19.5 us: per_device(): gathered = jnp.stack([lower, upper], axis=position)]
    dynamic_slice x2 -> x0, local copies, waits for them, and re-layouts: 25 us -> none  [the longest x1 20.4 us: per_device(): lax.dynamic_index_in_dim(column_view, bit_value, axis_index, keepdims=False)]
    ppermute x4 -> x24, starting transfers between devices: 7.3 us -> 27.8 us  [from_partner(): return lax.ppermute(block, axis, route)]
    broadcast_in_dim x3 -> x0, local copies, waits for them, and re-layouts: 19 us -> none  [the longest x2 12.5 us: per_device(): jnp.where(targets == target_low, pieces[0][None], jnp.where(targets == ta...]
  transfers between devices with their start and end apart: 5 -> 39, of which waited for: 5 -> 20; matrix products, arithmetic and copies ran while one was open for 9% -> 20% of each run, Pallas kernels for 0% -> 0%
where the time goes in v1:
time: 568 us; the launch traced here: 557 us
  waiting for transfers between devices  354 us (62%)
  matrix products  55.5 us (10%)
  other arithmetic  54.1 us (10%)
  starting transfers between devices  45.7 us (8%)
  between operations  26.1 us (5%)
  local copies, waits for them, and re-layouts  22 us (4%)
    ppermute x24, waiting for transfers between devices, from_partner(): return lax.ppermute(block, axis, route)  285 us
    ppermute x15, waiting for transfers between devices, from_offset(): return lax.ppermute(block, axis, [(i, i ^ offset) for i in range(count)])  68.7 us
    dot_general x20, matrix products, project(): jnp.dot(token_blocks[want, number], block, preferred_element_type=jnp.flo...  55.5 us
    ppermute x24, starting transfers between devices, from_partner(): return lax.ppermute(block, axis, route)  27.8 us
    ppermute x15, starting transfers between devices, from_offset(): return lax.ppermute(block, axis, [(i, i ^ offset) for i in range(count)])  17.9 us
    unnamed x127, local copies, waits for them, and re-layouts  13.2 us
    select_n x6, other arithmetic, to_groups(): chosen = jnp.where(target_low == row_index ^ offset, low, high)  12.6 us
    select_n x5, other arithmetic, to_groups(): foreign = jnp.where(foreign_from == here ^ offset, sources[offset], foreign)  11.4 us
  transfers between devices with their start and end apart: 39, of which 20 were waited for; matrix products, arithmetic and copies ran while one was open for 20% of the time, Pallas kernels for 0%

profile of v1, /device:TPU:0, one launch (start us, length us, event | category | flops | bytes accessed | tf_op | source)
XLA Modules:
  0.0 557.2 jit_solution(7053501030112534697)
XLA Ops:
  14.9 4.6 dynamic-slice_bitcast_fusion
  50.4 8.7 %collective-permute-done.22 = bf16[2048,128]{1,0:T(8,128)(2,1)} collective-permute-done((bf16[2048,128]{1,0:T(8,128)(2,1)}, bf16[2048,128]{1,0:T(8,128)(2,1)}, u32[]{:S(2)}, u32[]{:S(2)}) %collective-permute-start.22) | collective-permute-done | bytes 524320 | tf_op jit(solution)/shard_map/ppermute | solution.py:24
  72.3 7.7 %collective-permute-done.23 = bf16[2048,128]{1,0:T(8,128)(2,1)S(1)} collective-permute-done((bf16[2048,128]{1,0:T(8,128)(2,1)S(1)}, bf16[2048,128]{1,0:T(8,128)(2,1)S(1)}, u32[]{:S(2)}, u32[]{:S(2)}) %collective-permute-start.23) | collective-permute-done | bytes 524320 | tf_op jit(solution)/shard_map/ppermute | solution.py:19
  83.5 9.9 %collective-permute-done.27 = bf16[128,4096]{1,0:T(8,128)(2,1)} collective-permute-done((bf16[128,4096]{1,0:T(8,128)(2,1)}, bf16[128,4096]{1,0:T(8,128)(2,1)}, u32[]{:S(2)}, u32[]{:S(2)}) %collective-permute-start.27) | collective-permute-done | bytes 1048608 | tf_op jit(solution)/shard_map/ppermute | solution.py:19
  96.7 19.3 %collective-permute-done.28 = bf16[128,4096]{1,0:T(8,128)(2,1)} collective-permute-done((bf16[128,4096]{1,0:T(8,128)(2,1)}, bf16[128,4096]{1,0:T(8,128)(2,1)}, u32[]{:S(2)}, u32[]{:S(2)}) %collective-permute-start.28) | collective-permute-done | bytes 1048608 | tf_op jit(solution)/shard_map/ppermute | solution.py:19
  129.0 22.0 %collective-permute-done.11 = bf16[2048,256]{1,0:T(8,128)(2,1)} collective-permute-done((bf16[2048,256]{1,0:T(8,128)(2,1)}, bf16[2048,256]{1,0:T(8,128)(2,1)}, u32[]{:S(2)}, u32[]{:S(2)}) %collective-permute-start.11) | collective-permute-done | bytes 1048608 | tf_op jit(solution)/shard_map/ppermute | solution.py:24
  151.0 20.2 %collective-permute-done.12 = bf16[2048,256]{1,0:T(8,128)(2,1)} collective-permute-done((bf16[2048,256]{1,0:T(8,128)(2,1)}, bf16[2048,256]{1,0:T(8,128)(2,1)}, u32[]{:S(2)}, u32[]{:S(2)}) %collective-permute-start.12) | collective-permute-done | bytes 1048608 | tf_op jit(solution)/shard_map/ppermute | solution.py:24
  188.9 14.2 %collective-permute-done.35 = f32[512,128]{0,1:T(8,128)} collective-permute-done((f32[512,128]{0,1:T(8,128)S(1)}, f32[512,128]{0,1:T(8,128)}, u32[]{:S(2)}, u32[]{:S(2)}) %collective-permute-start.35) | collective-permute-done | bytes 262176 | tf_op jit(solution)/shard_map/ppermute | solution.py:19
  205.2 3.9 fusion.42
  209.1 22.3 %collective-permute-done.37 = f32[512,128]{0,1:T(8,128)} collective-permute-done((f32[512,128]{0,1:T(8,128)}, f32[512,128]{0,1:T(8,128)}, u32[]{:S(2)}, u32[]{:S(2)}) %collective-permute-start.37) | collective-permute-done | bytes 262176 | tf_op jit(solution)/shard_map/ppermute | solution.py:19
  236.7 48.6 %collective-permute-done.19 = bf16[4096,128]{1,0:T(8,128)(2,1)} collective-permute-done((bf16[4096,128]{1,0:T(8,128)(2,1)}, bf16[4096,128]{1,0:T(8,128)(2,1)}, u32[]{:S(2)}, u32[]{:S(2)}) %collective-permute-start.19) | collective-permute-done | bytes 1048608 | tf_op jit(solution)/shard_map/ppermute | solution.py:19
  302.8 4.2 collective-permute-done.24
  309.8 4.4 collective-permute-done.36
  317.0 41.8 %collective-permute-done.38 = f32[512,128]{0,1:T(8,128)S(1)} collective-permute-done((f32[512,128]{0,1:T(8,128)S(1)}, f32[512,128]{0,1:T(8,128)S(1)}, u32[]{:S(2)}, u32[]{:S(2)}) %collective-permute-start.38) | collective-permute-done | bytes 262176 | tf_op jit(solution)/shard_map/ppermute | solution.py:19
  358.8 3.9 collective-permute-start.14
  369.1 14.5 %collective-permute-done.3 = bf16[2,2048,256]{2,1,0:T(8,128)(2,1)} collective-permute-done((bf16[2,2048,256]{2,1,0:T(8,128)(2,1)S(1)}, bf16[2,2048,256]{2,1,0:T(8,128)(2,1)}, u32[]{:S(2)}, u32[]{:S(2)}) %collective-permute-start.3) | collective-permute-done | bytes 2097184 | tf_op jit(solution)/shard_map/ppermute | solution.py:24
  389.2 57.4 %collective-permute-done.9 = bf16[4096,256]{1,0:T(8,128)(2,1)} collective-permute-done((bf16[4096,256]{1,0:T(8,128)(2,1)}, bf16[4096,256]{1,0:T(8,128)(2,1)}, u32[]{:S(2)}, u32[]{:S(2)}) %collective-permute-start.9) | collective-permute-done | bytes 2097184 | tf_op jit(solution)/shard_map/ppermute | solution.py:19
  451.6 38.3 %collective-permute-done.14 = bf16[4096,256]{1,0:T(8,128)(2,1)} collective-permute-done((bf16[4096,256]{1,0:T(8,128)(2,1)}, bf16[4096,256]{1,0:T(8,128)(2,1)}, u32[]{:S(2)}, u32[]{:S(2)}) %collective-permute-start.14) | collective-permute-done | bytes 2097184 | tf_op jit(solution)/shard_map/ppermute | solution.py:19
  489.9 3.7 fusion.95
  495.6 5.5 collective-permute-done.32
  501.1 4.4 fusion.33
  505.5 4.5 broadcast_select_fusion.11
  512.2 4.2 fusion.39
  541.6 9.3 %collective-permute-done.29 = f32[512,256]{0,1:T(8,128)S(1)} collective-permute-done((f32[512,256]{0,1:T(8,128)S(1)}, f32[512,256]{0,1:T(8,128)S(1)}, u32[]{:S(2)}, u32[]{:S(2)}) %collective-permute-start.29) | collective-permute-done | bytes 524320 | tf_op jit(solution)/shard_map/ppermute | solution.py:19
  (258 shorter events, 153.4 us)
Async XLA Ops:
  19.4 49.4 %collective-permute-start.25 = (bf16[128,4096]{1,0:T(8,128)(2,1)}, bf16[128,4096]{1,0:T(8,128)(2,1)}, u32[]{:S(2)}, u32[]{:S(2)}) collective-permute-start(bf16[128,4096]{1,0:T(8,128)(2,1)} %get-tuple-element.107), channel_id=1, source_target_pairs={{0,2},{2,0},{1,3},{3,1},{4,6},{6,4},{5,7},{7,5},{8,10},{10,8},{9,1... | collective-permute-start | bytes 3145736 | tf_op jit(solution)/shard_map/ppermute | solution.py:19
  45.5 36.2 %collective-permute-start.26 = (bf16[128,4096]{1,0:T(8,128)(2,1)}, bf16[128,4096]{1,0:T(8,128)(2,1)}, u32[]{:S(2)}, u32[]{:S(2)}) collective-permute-start(bf16[128,4096]{1,0:T(8,128)(2,1)} %get-tuple-element.106), channel_id=1, source_target_pairs={{0,2},{2,0},{1,3},{3,1},{4,6},{6,4},{5,7},{7,5},{8,10},{10,8},{9,1... | collective-permute-start | bytes 3145736 | tf_op jit(solution)/shard_map/ppermute | solution.py:19
  48.3 45.2 %collective-permute-start.27 = (bf16[128,4096]{1,0:T(8,128)(2,1)}, bf16[128,4096]{1,0:T(8,128)(2,1)}, u32[]{:S(2)}, u32[]{:S(2)}) collective-permute-start(bf16[128,4096]{1,0:T(8,128)(2,1)} %get-tuple-element.105), channel_id=1, source_target_pairs={{0,2},{2,0},{1,3},{3,1},{4,6},{6,4},{5,7},{7,5},{8,10},{10,8},{9,1... | collective-permute-start | bytes 3145736 | tf_op jit(solution)/shard_map/ppermute | solution.py:19
  59.1 56.9 %collective-permute-start.28 = (bf16[128,4096]{1,0:T(8,128)(2,1)}, bf16[128,4096]{1,0:T(8,128)(2,1)}, u32[]{:S(2)}, u32[]{:S(2)}) collective-permute-start(bf16[128,4096]{1,0:T(8,128)(2,1)} %get-tuple-element.104), channel_id=1, source_target_pairs={{0,2},{2,0},{1,3},{3,1},{4,6},{6,4},{5,7},{7,5},{8,10},{10,8},{9,1... | collective-permute-start | bytes 3145736 | tf_op jit(solution)/shard_map/ppermute | solution.py:19
  68.8 51.7 %collective-permute-start.5 = (bf16[2048,256]{1,0:T(8,128)(2,1)S(1)}, bf16[2048,256]{1,0:T(8,128)(2,1)}, u32[]{:S(2)}, u32[]{:S(2)}) collective-permute-start(bf16[2048,256]{1,0:T(8,128)(2,1)S(1)} %copy-done.30), channel_id=1, source_target_pairs={{0,8},{8,0},{16,24},{24,16},{1,9},{9,1},{17,25},{25,17},{2,10},{10... | collective-permute-start | bytes 3145736 | tf_op jit(solution)/shard_map/ppermute | solution.py:24
  80.0 43.2 %collective-permute-start.6 = (bf16[2048,256]{1,0:T(8,128)(2,1)S(1)}, bf16[2048,256]{1,0:T(8,128)(2,1)S(1)}, u32[]{:S(2)}, u32[]{:S(2)}) collective-permute-start(bf16[2048,256]{1,0:T(8,128)(2,1)S(1)} %copy-done.29), channel_id=1, source_target_pairs={{0,16},{8,24},{16,0},{24,8},{1,17},{9,25},{17,1},{25,9},{2,18},{10... | collective-permute-start | bytes 3145736 | tf_op jit(solution)/shard_map/ppermute | solution.py:24
  81.7 46.3 %collective-permute-start.7 = (bf16[2048,256]{1,0:T(8,128)(2,1)S(1)}, bf16[2048,256]{1,0:T(8,128)(2,1)S(1)}, u32[]{:S(2)}, u32[]{:S(2)}) collective-permute-start(bf16[2048,256]{1,0:T(8,128)(2,1)S(1)} %copy-done.31), channel_id=1, source_target_pairs={{0,24},{8,16},{16,8},{24,0},{1,25},{9,17},{17,9},{25,1},{2,26},{10... | collective-permute-start | bytes 3145736 | tf_op jit(solution)/shard_map/ppermute | solution.py:24
  120.5 50.7 %collective-permute-start.12 = (bf16[2048,256]{1,0:T(8,128)(2,1)}, bf16[2048,256]{1,0:T(8,128)(2,1)}, u32[]{:S(2)}, u32[]{:S(2)}) collective-permute-start(bf16[2048,256]{1,0:T(8,128)(2,1)} %get-tuple-element.115), channel_id=1, source_target_pairs={{0,24},{8,16},{16,8},{24,0},{1,25},{9,17},{17,9},{25,1},{2,26},{10... | collective-permute-start | bytes 3145736 | tf_op jit(solution)/shard_map/ppermute | solution.py:24
  123.2 165.4 %collective-permute-start = (bf16[2,2048,256]{2,1,0:T(8,128)(2,1)}, bf16[2,2048,256]{2,1,0:T(8,128)(2,1)}, u32[]{:S(2)}, u32[]{:S(2)}) collective-permute-start(bf16[2,2048,256]{2,1,0:T(8,128)(2,1)} %get-tuple-element.123), channel_id=1, source_target_pairs={{0,4},{4,0},{1,5},{5,1},{2,6},{6,2},{3,7},{7,3},{8,12},{12,8},{9,1... | collective-permute-start | bytes 6291464 | tf_op jit(solution)/shard_map/ppermute | solution.py:19
  171.2 114.1 %collective-permute-start.19 = (bf16[4096,128]{1,0:T(8,128)(2,1)}, bf16[4096,128]{1,0:T(8,128)(2,1)}, u32[]{:S(2)}, u32[]{:S(2)}) collective-permute-start(bf16[4096,128]{1,0:T(8,128)(2,1)} %pad_maximum_fusion.4), channel_id=1, source_target_pairs={{0,4},{4,0},{1,5},{5,1},{2,6},{6,2},{3,7},{7,3},{8,12},{12,8},{9,1... | collective-permute-start | bytes 3145736 | tf_op jit(solution)/shard_map/ppermute | solution.py:19
  174.2 132.7 %collective-permute-start.24 = (bf16[4096,128]{1,0:T(8,128)(2,1)}, bf16[4096,128]{1,0:T(8,128)(2,1)}, u32[]{:S(2)}, u32[]{:S(2)}) collective-permute-start(bf16[4096,128]{1,0:T(8,128)(2,1)} %pad_maximum_fusion.5), channel_id=1, source_target_pairs={{0,4},{4,0},{1,5},{5,1},{2,6},{6,2},{3,7},{7,3},{8,12},{12,8},{9,1... | collective-permute-start | bytes 3145736 | tf_op jit(solution)/shard_map/ppermute | solution.py:19
  174.6 56.8 %collective-permute-start.37 = (f32[512,128]{0,1:T(8,128)}, f32[512,128]{0,1:T(8,128)}, u32[]{:S(2)}, u32[]{:S(2)}) collective-permute-start(f32[512,128]{0,1:T(8,128)} %fusion.82), channel_id=1, source_target_pairs={{0,2},{2,0},{1,3},{3,1},{4,6},{6,4},{5,7},{7,5},{8,10},{10,8},{9,1... | collective-permute-start | bytes 786440 | tf_op jit(solution)/shard_map/ppermute | solution.py:19
  203.2 87.7 %collective-permute-start.8 = (bf16[2048,256]{1,0:T(8,128)(2,1)}, bf16[2048,256]{1,0:T(8,128)(2,1)S(1)}, u32[]{:S(2)}, u32[]{:S(2)}) collective-permute-start(bf16[2048,256]{1,0:T(8,128)(2,1)} %select_select_fusion.4), channel_id=1, source_target_pairs={{0,1},{1,0},{2,3},{3,2},{4,5},{5,4},{6,7},{7,6},{8,9},{9,8},{10,11... | collective-permute-start | bytes 3145736 | tf_op jit(solution)/shard_map/ppermute | solution.py:19
  231.4 65.6 %collective-permute-start.13 = (bf16[2048,256]{1,0:T(8,128)(2,1)S(1)}, bf16[2048,256]{1,0:T(8,128)(2,1)S(1)}, u32[]{:S(2)}, u32[]{:S(2)}) collective-permute-start(bf16[2048,256]{1,0:T(8,128)(2,1)S(1)} %copy-done.38), channel_id=1, source_target_pairs={{0,1},{1,0},{2,3},{3,2},{4,5},{5,4},{6,7},{7,6},{8,9},{9,8},{10,11... | collective-permute-start | bytes 3145736 | tf_op jit(solution)/shard_map/ppermute | solution.py:19
  290.8 76.2 %collective-permute-start.1 = (bf16[2,2048,256]{2,1,0:T(8,128)(2,1)S(1)}, bf16[2,2048,256]{2,1,0:T(8,128)(2,1)}, u32[]{:S(2)}, u32[]{:S(2)}) collective-permute-start(bf16[2,2048,256]{2,1,0:T(8,128)(2,1)S(1)} %get-tuple-element.125), channel_id=1, source_target_pairs={{0,8},{8,0},{16,24},{24,16},{1,9},{9,1},{17,25},{25,17},{2,10},{10... | collective-permute-start | bytes 6291464 | tf_op jit(solution)/shard_map/ppermute | solution.py:24
  290.9 76.1 %collective-permute-start.2 = (bf16[2,2048,256]{2,1,0:T(8,128)(2,1)S(1)}, bf16[2,2048,256]{2,1,0:T(8,128)(2,1)}, u32[]{:S(2)}, u32[]{:S(2)}) collective-permute-start(bf16[2,2048,256]{2,1,0:T(8,128)(2,1)S(1)} %get-tuple-element.124), channel_id=1, source_target_pairs={{0,16},{8,24},{16,0},{24,8},{1,17},{9,25},{17,1},{25,9},{2,18},{10... | collective-permute-start | bytes 6291464 | tf_op jit(solution)/shard_map/ppermute | solution.py:24
  297.0 86.6 %collective-permute-start.3 = (bf16[2,2048,256]{2,1,0:T(8,128)(2,1)S(1)}, bf16[2,2048,256]{2,1,0:T(8,128)(2,1)}, u32[]{:S(2)}, u32[]{:S(2)}) collective-permute-start(bf16[2,2048,256]{2,1,0:T(8,128)(2,1)S(1)} %get-tuple-element.101), channel_id=1, source_target_pairs={{0,24},{8,16},{16,8},{24,0},{1,25},{9,17},{17,9},{25,1},{2,26},{10... | collective-permute-start | bytes 6291464 | tf_op jit(solution)/shard_map/ppermute | solution.py:24
  307.0 139.6 %collective-permute-start.9 = (bf16[4096,256]{1,0:T(8,128)(2,1)}, bf16[4096,256]{1,0:T(8,128)(2,1)}, u32[]{:S(2)}, u32[]{:S(2)}) collective-permute-start(bf16[4096,256]{1,0:T(8,128)(2,1)} %pad_maximum_fusion.2), channel_id=1, source_target_pairs={{0,4},{4,0},{1,5},{5,1},{2,6},{6,2},{3,7},{7,3},{8,12},{12,8},{9,1... | collective-permute-start | bytes 6291464 | tf_op jit(solution)/shard_map/ppermute | solution.py:19
  314.1 44.6 %collective-permute-start.38 = (f32[512,128]{0,1:T(8,128)S(1)}, f32[512,128]{0,1:T(8,128)S(1)}, u32[]{:S(2)}, u32[]{:S(2)}) collective-permute-start(f32[512,128]{0,1:T(8,128)S(1)} %fusion.97), channel_id=1, source_target_pairs={{0,2},{2,0},{1,3},{3,1},{4,6},{6,4},{5,7},{7,5},{8,10},{10,8},{9,1... | collective-permute-start | bytes 786440 | tf_op jit(solution)/shard_map/ppermute | solution.py:19
  358.8 131.1 %collective-permute-start.14 = (bf16[4096,256]{1,0:T(8,128)(2,1)}, bf16[4096,256]{1,0:T(8,128)(2,1)}, u32[]{:S(2)}, u32[]{:S(2)}) collective-permute-start(bf16[4096,256]{1,0:T(8,128)(2,1)} %pad_maximum_fusion.3), channel_id=1, source_target_pairs={{0,4},{4,0},{1,5},{5,1},{2,6},{6,2},{3,7},{7,3},{8,12},{12,8},{9,1... | collective-permute-start | bytes 6291464 | tf_op jit(solution)/shard_map/ppermute | solution.py:19
  367.0 138.5 %collective-permute-start.31 = (f32[512,256]{0,1:T(8,128)}, f32[512,256]{0,1:T(8,128)}, u32[]{:S(2)}, u32[]{:S(2)}) collective-permute-start(f32[512,256]{0,1:T(8,128)} %fusion.88), channel_id=1, source_target_pairs={{0,2},{2,0},{1,3},{3,1},{4,6},{6,4},{5,7},{7,5},{8,10},{10,8},{9,1... | collective-permute-start | bytes 1572872 | tf_op jit(solution)/shard_map/ppermute | solution.py:19
  367.0 149.3 %collective-permute-start.33 = (f32[512,256]{0,1:T(8,128)}, f32[512,256]{0,1:T(8,128)}, u32[]{:S(2)}, u32[]{:S(2)}) collective-permute-start(f32[512,256]{0,1:T(8,128)} %fusion.87), channel_id=1, source_target_pairs={{0,2},{2,0},{1,3},{3,1},{4,6},{6,4},{5,7},{7,5},{8,10},{10,8},{9,1... | collective-permute-start | bytes 1572872 | tf_op jit(solution)/shard_map/ppermute | solution.py:19
  389.1 130.4 %collective-permute-start.4 = (bf16[2,2048,256]{2,1,0:T(8,128)(2,1)}, bf16[2,2048,256]{2,1,0:T(8,128)(2,1)}, u32[]{:S(2)}, u32[]{:S(2)}) collective-permute-start(bf16[2,2048,256]{2,1,0:T(8,128)(2,1)} %select_select_fusion), channel_id=1, source_target_pairs={{0,1},{1,0},{2,3},{3,2},{4,5},{5,4},{6,7},{7,6},{8,9},{9,8},{10,11... | collective-permute-start | bytes 6291464 | tf_op jit(solution)/shard_map/ppermute | solution.py:19
  450.3 50.8 %collective-permute-start.32 = (f32[512,256]{0,1:T(8,128)}, f32[512,256]{0,1:T(8,128)}, u32[]{:S(2)}, u32[]{:S(2)}) collective-permute-start(f32[512,256]{0,1:T(8,128)} %fusion.94), channel_id=1, source_target_pairs={{0,2},{2,0},{1,3},{3,1},{4,6},{6,4},{5,7},{7,5},{8,10},{10,8},{9,1... | collective-permute-start | bytes 1572872 | tf_op jit(solution)/shard_map/ppermute | solution.py:19
  (75 other events, 1729.8 us)
